TPU v7x, 32 devices: a whole 2x2x4 slice. The times are simulated.
32 devices in a mesh: blk: 8 (over z, x), lane: 4 (over y, core).
Axes of the slice: x: 2, y: 2, z: 4, core: 2. Of those that a mesh axis runs over, the one named last changes fastest.
Arguments:
- left_factor: bfloat16 [4096, 512], P('blk'), may hold values from -6 to 6
- right_factor: bfloat16 [4, 4096, 512], P('lane', 'blk'), may hold values from -6 to 6
- observed: bfloat16 [4, 4, 512, 4096], P('lane', None, None, 'blk'), may hold values from -6 to 6
- row_codes: int32 [4096], P('blk'), may hold values from 0 to 1073741823
- shift_codes: int32 [4, 4, 4096], P('lane', None, 'blk'), may hold values from 0 to 29
Outputs:
- left_out: bfloat16 [4096, 512], P('blk')
- right_out: bfloat16 [4, 4096, 512], P('lane', 'blk')
Inputs may be any that keep to these rules, and one draw needn't show every extreme that they name: `row_codes`: each row's word carries thirty independent sampling bits. `shift_codes`: A bit number for each lane, cycle step and visited tile entry column.
All inputs are finite; a program needn't handle non-finite values.
Results may differ from a plain program's by a relative error of at most 0.013.
Values may be sent and summed in bfloat16 or wider, within the bound.
A program may use at most 64 MiB of HBM per device.

v0:
```python
import math
import jax
import jax.numpy as jnp
from jax import lax
from jax.sharding import PartitionSpec as P

step_right = 0.25
step_left = 0.1


def passed_along(value, axis, steps):
    count = lax.axis_size(axis)
    pairs = [(source, (source + steps) % count) for source in range(count)]
    return lax.ppermute(value, axis, pairs)


def visit_tile(right_part, left_factor, target, row_codes, shifts, root_scale):
    predicted = (
        lax.dot_general(
            right_part, left_factor, (((1,), (1,)), ((), ())), preferred_element_type=jnp.float32
        )
        * root_scale
    )
    sample_bits = jnp.right_shift(row_codes[None, :], shifts[:, None]) & 1
    error_tile = jnp.where(sample_bits == 1, predicted - target.astype(jnp.float32), 0.0).astype(
        jnp.bfloat16
    )
    grad_right = jnp.dot(error_tile, left_factor, preferred_element_type=jnp.float32)
    grad_left = lax.dot_general(
        error_tile, right_part, (((0,), (0,)), ((), ())), preferred_element_type=jnp.float32
    )
    updated = (right_part.astype(jnp.float32) - step_right * root_scale * grad_right).astype(
        jnp.bfloat16
    )
    return (updated, grad_left)


def local(left_factor, right_factor, observed, row_codes, shift_codes):
    rank_size = left_factor.shape[1]
    root_scale = 1.0 / math.sqrt(rank_size)
    cycle_steps = observed.shape[1]
    column_count = observed.shape[2]
    right_now = right_factor[0]
    grad_sum = jnp.zeros(left_factor.shape, jnp.float32)
    for cycle_step in range(cycle_steps):
        target = observed[0, cycle_step]
        shifts = shift_codes[0, cycle_step]
        last_step = cycle_step + 1 == cycle_steps
        half_cols = column_count // 2
        pieces = []
        for portion in range(2):
            first_col = portion * half_cols
            updated, grad_left = visit_tile(
                right_now[first_col : first_col + half_cols],
                left_factor,
                target[first_col : first_col + half_cols],
                row_codes,
                shifts[first_col : first_col + half_cols],
                root_scale,
            )
            grad_sum = grad_sum + grad_left
            pieces.append(updated if last_step else passed_along(updated, "blk", 1))
        right_now = jnp.concatenate(pieces, axis=0)
    summed = lax.psum(grad_sum.astype(jnp.bfloat16), "lane").astype(jnp.float32)
    left_out = (left_factor.astype(jnp.float32) - step_left * root_scale * summed).astype(
        jnp.bfloat16
    )
    return (left_out, right_now[None])


def solution(mesh):
    in_specs = (
        P("blk", None),
        P("lane", "blk", None),
        P("lane", None, None, "blk"),
        P("blk"),
        P("lane", None, "blk"),
    )
    out_specs = (P("blk", None), P("lane", "blk", None))
    return jax.shard_map(local, mesh=mesh, in_specs=in_specs, out_specs=out_specs, check_vma=False)
```

profile of v0, /device:TPU:0, one launch (start us, length us, event | category | flops | bytes accessed | tf_op | source)
XLA Modules:
  0.0 94.1 jit_solution(8575521751137089536)
XLA Ops:
  7.2 0.0 copy-start
  7.2 0.0 copy-start.3
  7.2 0.0 copy-start.1
  7.2 0.0 all-reduce.2.cloned.1.call-start
  7.2 0.0 copy-start.2
  7.3 0.9 fusion.43
  8.2 1.6 %fusion.27 = bf16[256,512]{1,0:T(8,128)(2,1)S(1)} fusion(bf16[512,512]{1,0:T(8,128)(2,1)} %param.5, bf16[1,4,512,512]{3,2,1,0:T(8,128)(2,1)} %param.7, s32[256]{0:T(256)S(1)} %bitcast.97, s32[512]{0:T(512)} %param.8, bf16[1,512,512]{2,1,0:T(8,128)(2,1)} %param.6), kind=kOutput, calls=%fused_computation.45 | convolution fusion | flops 135266304 | bytes 1313792 | tf_op jit(solution)/shard_map/dot_general | solution.py:19
  9.8 0.0 copy-done
  9.8 0.3 fusion.25
  10.1 3.0 %collective-permute-start.1 = (bf16[256,512]{1,0:T(8,128)(2,1)S(1)}, bf16[256,512]{1,0:T(8,128)(2,1)S(1)}, u32[]{:S(2)}, u32[]{:S(2)}) collective-permute-start(bf16[256,512]{1,0:T(8,128)(2,1)S(1)} %fusion.25), channel_id=1, source_target_pairs={{0,4},{4,8},{8,12},{12,16},{16,20},{20,24},{24,28},{28,0},{1,5},{5... | collective-permute-start | bytes 786440 | tf_op jit(solution)/shard_map/ppermute | solution.py:14
  13.1 0.0 copy-done.3
  13.1 0.4 fusion.26
  13.5 0.3 fusion.24
  13.8 1.6 %collective-permute-start = (bf16[256,512]{1,0:T(8,128)(2,1)S(1)}, bf16[256,512]{1,0:T(8,128)(2,1)S(1)}, u32[]{:S(2)}, u32[]{:S(2)}) collective-permute-start(bf16[256,512]{1,0:T(8,128)(2,1)S(1)} %fusion.24), channel_id=1, source_target_pairs={{0,4},{4,8},{8,12},{12,16},{16,20},{20,24},{24,28},{28,0},{1,5},{5... | collective-permute-start | bytes 786440 | tf_op jit(solution)/shard_map/ppermute | solution.py:14
  15.4 0.3 fusion.36
  15.7 0.3 convolution_add_fusion.1
  16.1 7.2 %collective-permute-done.1 = bf16[256,512]{1,0:T(8,128)(2,1)S(1)} collective-permute-done((bf16[256,512]{1,0:T(8,128)(2,1)S(1)}, bf16[256,512]{1,0:T(8,128)(2,1)S(1)}, u32[]{:S(2)}, u32[]{:S(2)}) %collective-permute-start.1) | collective-permute-done | bytes 262176 | tf_op jit(solution)/shard_map/ppermute | solution.py:14
  23.3 0.4 fusion.29
  23.7 0.3 subtract_convert_fusion.5
  24.0 0.1 collective-permute-start.3
  24.1 4.3 %collective-permute-done = bf16[256,512]{1,0:T(8,128)(2,1)S(1)} collective-permute-done((bf16[256,512]{1,0:T(8,128)(2,1)S(1)}, bf16[256,512]{1,0:T(8,128)(2,1)S(1)}, u32[]{:S(2)}, u32[]{:S(2)}) %collective-permute-start) | collective-permute-done | bytes 262176 | tf_op jit(solution)/shard_map/ppermute | solution.py:14
  28.4 0.4 fusion.28
  28.8 0.3 subtract_convert_fusion.6
  29.1 0.1 collective-permute-start.2
  29.1 0.3 fusion.44
  29.5 4.5 %collective-permute-done.3 = bf16[256,512]{1,0:T(8,128)(2,1)S(1)} collective-permute-done((bf16[256,512]{1,0:T(8,128)(2,1)S(1)}, bf16[256,512]{1,0:T(8,128)(2,1)S(1)}, u32[]{:S(2)}, u32[]{:S(2)}) %collective-permute-start.3) | collective-permute-done | bytes 262176 | tf_op jit(solution)/shard_map/ppermute | solution.py:14
  34.0 0.4 fusion.31
  34.4 0.3 subtract_convert_fusion.3
  34.7 0.1 collective-permute-start.5
  34.8 6.2 %collective-permute-done.2 = bf16[256,512]{1,0:T(8,128)(2,1)S(1)} collective-permute-done((bf16[256,512]{1,0:T(8,128)(2,1)S(1)}, bf16[256,512]{1,0:T(8,128)(2,1)S(1)}, u32[]{:S(2)}, u32[]{:S(2)}) %collective-permute-start.2) | collective-permute-done | bytes 262176 | tf_op jit(solution)/shard_map/ppermute | solution.py:14
  41.0 0.4 fusion.30
  41.4 0.3 subtract_convert_fusion.4
  41.7 0.1 collective-permute-start.4
  41.8 0.3 fusion.45
  42.1 0.3 fusion.46
  42.4 8.4 %collective-permute-done.4 = bf16[256,512]{1,0:T(8,128)(2,1)S(1)} collective-permute-done((bf16[256,512]{1,0:T(8,128)(2,1)S(1)}, bf16[256,512]{1,0:T(8,128)(2,1)S(1)}, u32[]{:S(2)}, u32[]{:S(2)}) %collective-permute-start.4) | collective-permute-done | bytes 262176 | tf_op jit(solution)/shard_map/ppermute | solution.py:14
  50.8 0.4 fusion.32
  51.2 0.3 fusion.47
  51.5 0.0 collective-permute-done.5
  51.5 0.4 fusion.33
  51.9 0.3 fusion.48
  52.2 1.3 %fusion.5 = bf16[512,512]{1,0:T(8,128)(2,1)} fusion(f32[512,512]{1,0:T(8,128)S(1)} %fusion.48, f32[512,512]{1,0:T(8,128)S(1)} %fusion.47, f32[512,512]{1,0:T(8,128)S(1)} %fusion.46, f32[512,512]{1,0:T(8,128)S(1)} %fusion.45, f32[512,512]{1,0:T(8,128)S(1)} %fusion.44, f32[512,512]{1,0:T(8,128)S(1)} %convolution_add_fusion.1, ...), kind=kOutput, calls=%fused_computation.7 | convolution fusion | flops 136052736 | bytes 7340032 | tf_op jit(solution)/shard_map/dot_general | solution.py:29
  53.5 0.0 all-reduce.2.cloned.1.call-update
  53.5 0.3 subtract_convert_fusion.1
  53.9 0.3 subtract_convert_fusion.2
  54.2 0.8 maximum_bitcast_fusion
  55.0 30.3 %all-reduce.2.cloned.1.call-done = bf16[512,512]{1,0:T(8,128)(2,1)} async-done(((bf16[512,512]{1,0:T(8,128)(2,1)}), bf16[512,512]{1,0:T(8,128)(2,1)}) %all-reduce.2.cloned.1.call-update) | async-done | bytes 524304 | tf_op jit(solution)/shard_map/psum | solution.py:64
  85.3 2.0 %subtract_convert_fusion = bf16[512,512]{1,0:T(8,128)(2,1)} fusion(bf16[512,512]{1,0:T(8,128)(2,1)} %all-reduce.2.cloned.1.call-done, bf16[512,512]{1,0:T(8,128)(2,1)S(1)} %copy-done), kind=kLoop, calls=%fused_computation.52 | loop fusion | flops 1310720 | bytes 1572864 | tf_op jit(solution)/shard_map/convert_element_type | solution.py:65
  (2 shorter events, 0.0 us)
Async XLA Ops:
  7.2 2.6 %copy-start = (bf16[512,512]{1,0:T(8,128)(2,1)S(1)}, bf16[512,512]{1,0:T(8,128)(2,1)}, u32[]{:S(2)}) copy-start(bf16[512,512]{1,0:T(8,128)(2,1)} %param.5) | copy-start | bytes 1572868
  7.2 5.9 %copy-start.3 = (s32[512]{0:T(512)S(1)}, s32[512]{0:T(512)}, u32[]{:S(2)}) copy-start(s32[512]{0:T(512)} %param.8) | copy-start | bytes 6148
  7.2 2.6 %copy-start.1 = (bf16[1,512,512]{2,1,0:T(8,128)(2,1)S(1)}, bf16[1,512,512]{2,1,0:T(8,128)(2,1)}, u32[]{:S(2)}) copy-start(bf16[1,512,512]{2,1,0:T(8,128)(2,1)} %param.6) | copy-start | bytes 1572868
  7.2 78.1 %all-reduce.2.cloned.1.call-start = ((), (), s32[]{:S(2)}) async-start(), calls=%async_computation | async-start | bytes 1048576 | tf_op jit(solution)/shard_map/psum | solution.py:64
  7.2 5.9 %copy-start.2 = (bf16[1,4,512,512]{3,2,1,0:T(8,128)(2,1)S(1)}, bf16[1,4,512,512]{3,2,1,0:T(8,128)(2,1)}, u32[]{:S(2)}) copy-start(bf16[1,4,512,512]{3,2,1,0:T(8,128)(2,1)} %param.7) | copy-start | bytes 6291460
  10.1 13.2 %collective-permute-start.1 = (bf16[256,512]{1,0:T(8,128)(2,1)S(1)}, bf16[256,512]{1,0:T(8,128)(2,1)S(1)}, u32[]{:S(2)}, u32[]{:S(2)}) collective-permute-start(bf16[256,512]{1,0:T(8,128)(2,1)S(1)} %fusion.25), channel_id=1, source_target_pairs={{0,4},{4,8},{8,12},{12,16},{16,20},{20,24},{24,28},{28,0},{1,5},{5... | collective-permute-start | bytes 786440 | tf_op jit(solution)/shard_map/ppermute | solution.py:14
  13.8 14.6 %collective-permute-start = (bf16[256,512]{1,0:T(8,128)(2,1)S(1)}, bf16[256,512]{1,0:T(8,128)(2,1)S(1)}, u32[]{:S(2)}, u32[]{:S(2)}) collective-permute-start(bf16[256,512]{1,0:T(8,128)(2,1)S(1)} %fusion.24), channel_id=1, source_target_pairs={{0,4},{4,8},{8,12},{12,16},{16,20},{20,24},{24,28},{28,0},{1,5},{5... | collective-permute-start | bytes 786440 | tf_op jit(solution)/shard_map/ppermute | solution.py:14
  24.0 10.0 %collective-permute-start.3 = (bf16[256,512]{1,0:T(8,128)(2,1)S(1)}, bf16[256,512]{1,0:T(8,128)(2,1)S(1)}, u32[]{:S(2)}, u32[]{:S(2)}) collective-permute-start(bf16[256,512]{1,0:T(8,128)(2,1)S(1)} %subtract_convert_fusion.5), channel_id=1, source_target_pairs={{0,4},{4,8},{8,12},{12,16},{16,20},{20,24},{24,28},{28,0},{1,5},{5... | collective-permute-start | bytes 786440 | tf_op jit(solution)/shard_map/ppermute | solution.py:14
  29.1 11.9 %collective-permute-start.2 = (bf16[256,512]{1,0:T(8,128)(2,1)S(1)}, bf16[256,512]{1,0:T(8,128)(2,1)S(1)}, u32[]{:S(2)}, u32[]{:S(2)}) collective-permute-start(bf16[256,512]{1,0:T(8,128)(2,1)S(1)} %subtract_convert_fusion.6), channel_id=1, source_target_pairs={{0,4},{4,8},{8,12},{12,16},{16,20},{20,24},{24,28},{28,0},{1,5},{5... | collective-permute-start | bytes 786440 | tf_op jit(solution)/shard_map/ppermute | solution.py:14
  34.7 16.8 %collective-permute-start.5 = (bf16[256,512]{1,0:T(8,128)(2,1)S(1)}, bf16[256,512]{1,0:T(8,128)(2,1)S(1)}, u32[]{:S(2)}, u32[]{:S(2)}) collective-permute-start(bf16[256,512]{1,0:T(8,128)(2,1)S(1)} %subtract_convert_fusion.3), channel_id=1, source_target_pairs={{0,4},{4,8},{8,12},{12,16},{16,20},{20,24},{24,28},{28,0},{1,5},{5... | collective-permute-start | bytes 786440 | tf_op jit(solution)/shard_map/ppermute | solution.py:14
  41.7 9.1 %collective-permute-start.4 = (bf16[256,512]{1,0:T(8,128)(2,1)S(1)}, bf16[256,512]{1,0:T(8,128)(2,1)S(1)}, u32[]{:S(2)}, u32[]{:S(2)}) collective-permute-start(bf16[256,512]{1,0:T(8,128)(2,1)S(1)} %subtract_convert_fusion.4), channel_id=1, source_target_pairs={{0,4},{4,8},{8,12},{12,16},{16,20},{20,24},{24,28},{28,0},{1,5},{5... | collective-permute-start | bytes 786440 | tf_op jit(solution)/shard_map/ppermute | solution.py:14
Sparse Core Ops, SparseCore 0:
  53.7 31.5 all-reduce.1
where the time goes:
time: 94.3 us; the launch traced here: 94.1 us
  waiting for transfers between devices  61.1 us (65%)
  between operations  14.3 us (15%)
  matrix products  10.2 us (11%)
  starting transfers between devices  4.89 us (5%)
  other arithmetic  2.82 us (3%)
  local copies, waits for them, and re-layouts  0.95 us (1%)
    ppermute x6, waiting for transfers between devices, passed_along(): return lax.ppermute(value, axis, pairs)  30.7 us
    psum x1, waiting for transfers between devices, local(): summed = lax.psum(grad_sum.astype(jnp.bfloat16), 'lane').astype(jnp.float32)  30.3 us
    ppermute x6, starting transfers between devices, passed_along(): return lax.ppermute(value, axis, pairs)  4.85 us
    dot_general x8, matrix products, visit_tile(): lax.dot_general(right_part, left_factor, (((1,), (1,)), ((), ())), prefer...  4.16 us
    dot_general x8, matrix products, visit_tile(): lax.dot_general(error_tile, right_part, (((0,), (0,)), ((), ())), preferr...  3.58 us
    dot_general x8, matrix products, visit_tile(): jnp.dot(error_tile, left_factor, preferred_element_type=jnp.float32)  2.42 us
    convert_element_type x1, other arithmetic, local(): (left_factor.astype(jnp.float32) - step_left * root_scale * summed).astyp...  1.99 us
  transfers between devices with their start and end apart: 7, of which 6 were waited for; matrix products, arithmetic and copies ran while one was open for 8% of the time, Pallas kernels for 0%

commit v1 on v0

--- a/solution.py
+++ b/solution.py
@@ -61,7 +61,9 @@
             grad_sum = grad_sum + grad_left
             pieces.append(updated if last_step else passed_along(updated, "blk", 1))
         right_now = jnp.concatenate(pieces, axis=0)
-    summed = lax.psum(grad_sum.astype(jnp.bfloat16), "lane").astype(jnp.float32)
+    summed = jnp.sum(lax.all_gather(grad_sum.astype(jnp.bfloat16), "lane"), axis=0).astype(
+        jnp.float32
+    )
     left_out = (left_factor.astype(jnp.float32) - step_left * root_scale * summed).astype(
         jnp.bfloat16
     )

time: 94.3 us -> 85.6 us (0.908)
  waiting for transfers between devices: 61.1 us -> 50.2 us
  other arithmetic: 2.82 us -> 3.96 us
    psum x1 -> x0, waiting for transfers between devices: 30.3 us -> none  [local(): summed = lax.psum(grad_sum.astype(jnp.bfloat16), 'lane').astype(jnp.float32)]
    all_gather x0 -> x1, waiting for transfers between devices: none -> 19.5 us  [local(): lax.all_gather(grad_sum.astype(jnp.bfloat16), 'lane')]
    reduce_sum x0 -> x1, other arithmetic: none -> 2.18 us  [local(): jnp.sum(lax.all_gather(grad_sum.astype(jnp.bfloat16), 'lane'), axis=0)]
    convert_element_type x1, other arithmetic: 1.99 us -> 0.95 us  [local(): (left_factor.astype(jnp.float32) - step_left * root_scale * summed).astyp...]
where the time goes in v1:
time: 85.6 us; the launch traced here: 85.4 us
  waiting for transfers between devices  50.2 us (59%)
  between operations  14.3 us (17%)
  matrix products  11.1 us (13%)
  starting transfers between devices  4.89 us (6%)
  other arithmetic  3.96 us (5%)
  local copies, waits for them, and re-layouts  0.95 us (1%)
    ppermute x6, waiting for transfers between devices, passed_along(): return lax.ppermute(value, axis, pairs)  30.8 us
    all_gather x1, waiting for transfers between devices, local(): lax.all_gather(grad_sum.astype(jnp.bfloat16), 'lane')  19.5 us
    dot_general x8, matrix products, visit_tile(): lax.dot_general(right_part, left_factor, (((1,), (1,)), ((), ())), prefer...  5.08 us
    ppermute x6, starting transfers between devices, passed_along(): return lax.ppermute(value, axis, pairs)  4.85 us
    dot_general x8, matrix products, visit_tile(): lax.dot_general(error_tile, right_part, (((0,), (0,)), ((), ())), preferr...  3.58 us
    dot_general x8, matrix products, visit_tile(): jnp.dot(error_tile, left_factor, preferred_element_type=jnp.float32)  2.44 us
    reduce_sum x1, other arithmetic, local(): jnp.sum(lax.all_gather(grad_sum.astype(jnp.bfloat16), 'lane'), axis=0)  2.18 us
  transfers between devices with their start and end apart: 7, of which 6 were waited for; matrix products, arithmetic and copies ran while one was open for 8% of the time, Pallas kernels for 0%

profile of v1, /device:TPU:0, one launch (start us, length us, event | category | flops | bytes accessed | tf_op | source)
XLA Modules:
  0.0 85.4 jit_solution(14675379530674145588)
XLA Ops:
  7.2 0.0 copy-start
  7.2 0.0 copy-start.3
  7.2 0.0 copy-start.1
  7.2 0.0 copy-start.2
  7.2 0.0 all-gather.3.cloned.1.call-start
  7.3 0.9 %fusion.43 = (s32[1,1,256]{2,1,0:T(1,128)S(1)}, s32[1,1,256]{2,1,0:T(1,128)S(1)}, s32[1,1,256]{2,1,0:T(1,128)S(1)}, s32[1,1,256]{2,1,0:T(1,128)S(1)}, s32[1,1,25...) fusion(s32[1,4,512]{2,1,0:T(4,128)} %param.9), kind=kLoop, calls=%fused_computation.77 | loop fusion | bytes 16384 | tf_op jit(solution)/shard_map/slice | solution.py:58
  8.2 1.6 %fusion.27 = bf16[256,512]{1,0:T(8,128)(2,1)S(1)} fusion(bf16[512,512]{1,0:T(8,128)(2,1)} %param.5, bf16[1,4,512,512]{3,2,1,0:T(8,128)(2,1)} %param.7, s32[256]{0:T(256)S(1)} %bitcast.99, s32[512]{0:T(512)} %param.8, bf16[1,512,512]{2,1,0:T(8,128)(2,1)} %param.6), kind=kOutput, calls=%fused_computation.45 | convolution fusion | flops 135266304 | bytes 1313792 | tf_op jit(solution)/shard_map/dot_general | solution.py:19
  9.8 0.0 copy-done
  9.8 0.3 fusion.25
  10.1 3.0 %collective-permute-start.1 = (bf16[256,512]{1,0:T(8,128)(2,1)S(1)}, bf16[256,512]{1,0:T(8,128)(2,1)S(1)}, u32[]{:S(2)}, u32[]{:S(2)}) collective-permute-start(bf16[256,512]{1,0:T(8,128)(2,1)S(1)} %fusion.25), channel_id=1, source_target_pairs={{0,4},{4,8},{8,12},{12,16},{16,20},{20,24},{24,28},{28,0},{1,5},{5... | collective-permute-start | bytes 786440 | tf_op jit(solution)/shard_map/ppermute | solution.py:14
  13.1 0.4 fusion.26
  13.5 0.3 fusion.24
  13.8 1.6 %collective-permute-start = (bf16[256,512]{1,0:T(8,128)(2,1)S(1)}, bf16[256,512]{1,0:T(8,128)(2,1)S(1)}, u32[]{:S(2)}, u32[]{:S(2)}) collective-permute-start(bf16[256,512]{1,0:T(8,128)(2,1)S(1)} %fusion.24), channel_id=1, source_target_pairs={{0,4},{4,8},{8,12},{12,16},{16,20},{20,24},{24,28},{28,0},{1,5},{5... | collective-permute-start | bytes 786440 | tf_op jit(solution)/shard_map/ppermute | solution.py:14
  15.4 0.3 fusion.36
  15.7 0.3 convolution_add_fusion.1
  16.1 7.2 %collective-permute-done.1 = bf16[256,512]{1,0:T(8,128)(2,1)S(1)} collective-permute-done((bf16[256,512]{1,0:T(8,128)(2,1)S(1)}, bf16[256,512]{1,0:T(8,128)(2,1)S(1)}, u32[]{:S(2)}, u32[]{:S(2)}) %collective-permute-start.1) | collective-permute-done | bytes 262176 | tf_op jit(solution)/shard_map/ppermute | solution.py:14
  23.3 0.4 fusion.29
  23.7 0.3 subtract_convert_fusion.5
  24.0 0.1 collective-permute-start.3
  24.1 4.3 %collective-permute-done = bf16[256,512]{1,0:T(8,128)(2,1)S(1)} collective-permute-done((bf16[256,512]{1,0:T(8,128)(2,1)S(1)}, bf16[256,512]{1,0:T(8,128)(2,1)S(1)}, u32[]{:S(2)}, u32[]{:S(2)}) %collective-permute-start) | collective-permute-done | bytes 262176 | tf_op jit(solution)/shard_map/ppermute | solution.py:14
  28.4 0.4 fusion.28
  28.8 0.3 subtract_convert_fusion.6
  29.1 0.1 collective-permute-start.2
  29.1 0.3 fusion.44
  29.5 4.5 %collective-permute-done.3 = bf16[256,512]{1,0:T(8,128)(2,1)S(1)} collective-permute-done((bf16[256,512]{1,0:T(8,128)(2,1)S(1)}, bf16[256,512]{1,0:T(8,128)(2,1)S(1)}, u32[]{:S(2)}, u32[]{:S(2)}) %collective-permute-start.3) | collective-permute-done | bytes 262176 | tf_op jit(solution)/shard_map/ppermute | solution.py:14
  34.0 0.4 fusion.31
  34.4 0.3 subtract_convert_fusion.3
  34.7 0.1 collective-permute-start.5
  34.8 6.2 %collective-permute-done.2 = bf16[256,512]{1,0:T(8,128)(2,1)S(1)} collective-permute-done((bf16[256,512]{1,0:T(8,128)(2,1)S(1)}, bf16[256,512]{1,0:T(8,128)(2,1)S(1)}, u32[]{:S(2)}, u32[]{:S(2)}) %collective-permute-start.2) | collective-permute-done | bytes 262176 | tf_op jit(solution)/shard_map/ppermute | solution.py:14
  41.0 0.4 fusion.30
  41.4 0.3 subtract_convert_fusion.4
  41.7 0.1 collective-permute-start.4
  41.8 0.3 fusion.45
  42.1 0.3 fusion.46
  42.4 8.4 %collective-permute-done.4 = bf16[256,512]{1,0:T(8,128)(2,1)S(1)} collective-permute-done((bf16[256,512]{1,0:T(8,128)(2,1)S(1)}, bf16[256,512]{1,0:T(8,128)(2,1)S(1)}, u32[]{:S(2)}, u32[]{:S(2)}) %collective-permute-start.4) | collective-permute-done | bytes 262176 | tf_op jit(solution)/shard_map/ppermute | solution.py:14
  50.8 0.4 fusion.32
  51.2 0.3 fusion.47
  51.5 0.0 collective-permute-done.5
  51.5 1.3 %fusion.33 = bf16[256,512]{1,0:T(8,128)(2,1)S(1)} fusion(bf16[256,512]{1,0:T(8,128)(2,1)S(1)} %collective-permute-done.5, bf16[512,512]{1,0:T(8,128)(2,1)S(1)} %copy-done, bf16[1,4,512,512]{3,2,1,0:T(8,128)(2,1)} %param.7, s32[256]{0:T(256)S(1)} %bitcast.92, s32[512]{0:T(512)S(1)} %copy-done.3), kind=kOutput, calls=%fused_computation.51 | convolution fusion | flops 135266304 | bytes 1313792 | tf_op jit(solution)/shard_map/dot_general | solution.py:19
  52.8 0.3 fusion.48
  53.2 1.3 %fusion.5 = bf16[512,512]{1,0:T(8,128)(2,1)} fusion(f32[512,512]{1,0:T(8,128)S(1)} %fusion.48, f32[512,512]{1,0:T(8,128)S(1)} %fusion.47, f32[512,512]{1,0:T(8,128)S(1)} %fusion.46, f32[512,512]{1,0:T(8,128)S(1)} %fusion.45, f32[512,512]{1,0:T(8,128)S(1)} %fusion.44, f32[512,512]{1,0:T(8,128)S(1)} %convolution_add_fusion.1, ...), kind=kOutput, calls=%fused_computation.7 | convolution fusion | flops 136052736 | bytes 7340032 | tf_op jit(solution)/shard_map/dot_general | solution.py:29
  54.5 0.0 all-gather.3.cloned.1.call-update
  54.5 0.3 subtract_convert_fusion.1
  54.8 0.3 subtract_convert_fusion.2
  55.1 0.8 maximum_bitcast_fusion
  55.9 19.5 %all-gather.3.cloned.1.call-done = bf16[2048,512]{1,0:T(8,128)(2,1)} async-done(((bf16[512,512]{1,0:T(8,128)(2,1)}), bf16[2048,512]{1,0:T(8,128)(2,1)}) %all-gather.3.cloned.1.call-update) | async-done | bytes 2097168 | tf_op jit(solution)/shard_map/all_gather | solution.py:64
  75.4 2.2 %reduce_sum.12 = bf16[512,512]{1,0:T(8,128)(2,1)S(1)} reduce(bf16[4,512,512]{2,1,0:T(8,128)(2,1)} %bitcast.91, bf16[]{:T(256)} %constant.10.clone.1), dimensions={0}, to_apply=%region_0.1 | reduce | flops 786432 | bytes 2621442 | tf_op jit(solution)/shard_map/reduce_sum | solution.py:64
  77.6 1.0 %subtract_convert_fusion = bf16[512,512]{1,0:T(8,128)(2,1)} fusion(bf16[512,512]{1,0:T(8,128)(2,1)S(1)} %reduce_sum.12, bf16[512,512]{1,0:T(8,128)(2,1)S(1)} %copy-done), kind=kLoop, calls=%fused_computation.52 | loop fusion | flops 1310720 | bytes 1572864 | tf_op jit(solution)/shard_map/convert_element_type | solution.py:67
  (3 shorter events, 0.0 us)
Async XLA Ops:
  7.2 2.6 %copy-start = (bf16[512,512]{1,0:T(8,128)(2,1)S(1)}, bf16[512,512]{1,0:T(8,128)(2,1)}, u32[]{:S(2)}) copy-start(bf16[512,512]{1,0:T(8,128)(2,1)} %param.5) | copy-start | bytes 1572868
  7.2 5.9 %copy-start.3 = (s32[512]{0:T(512)S(1)}, s32[512]{0:T(512)}, u32[]{:S(2)}) copy-start(s32[512]{0:T(512)} %param.8) | copy-start | bytes 6148
  7.2 2.6 %copy-start.1 = (bf16[1,512,512]{2,1,0:T(8,128)(2,1)S(1)}, bf16[1,512,512]{2,1,0:T(8,128)(2,1)}, u32[]{:S(2)}) copy-start(bf16[1,512,512]{2,1,0:T(8,128)(2,1)} %param.6) | copy-start | bytes 1572868
  7.2 5.9 %copy-start.2 = (bf16[1,4,512,512]{3,2,1,0:T(8,128)(2,1)S(1)}, bf16[1,4,512,512]{3,2,1,0:T(8,128)(2,1)}, u32[]{:S(2)}) copy-start(bf16[1,4,512,512]{3,2,1,0:T(8,128)(2,1)} %param.7) | copy-start | bytes 6291460
  7.2 68.2 %all-gather.3.cloned.1.call-start = ((), (), s32[]{:S(2)}) async-start(), calls=%async_computation | async-start | bytes 2621440 | tf_op jit(solution)/shard_map/all_gather | solution.py:64
  10.1 13.2 %collective-permute-start.1 = (bf16[256,512]{1,0:T(8,128)(2,1)S(1)}, bf16[256,512]{1,0:T(8,128)(2,1)S(1)}, u32[]{:S(2)}, u32[]{:S(2)}) collective-permute-start(bf16[256,512]{1,0:T(8,128)(2,1)S(1)} %fusion.25), channel_id=1, source_target_pairs={{0,4},{4,8},{8,12},{12,16},{16,20},{20,24},{24,28},{28,0},{1,5},{5... | collective-permute-start | bytes 786440 | tf_op jit(solution)/shard_map/ppermute | solution.py:14
  13.8 14.6 %collective-permute-start = (bf16[256,512]{1,0:T(8,128)(2,1)S(1)}, bf16[256,512]{1,0:T(8,128)(2,1)S(1)}, u32[]{:S(2)}, u32[]{:S(2)}) collective-permute-start(bf16[256,512]{1,0:T(8,128)(2,1)S(1)} %fusion.24), channel_id=1, source_target_pairs={{0,4},{4,8},{8,12},{12,16},{16,20},{20,24},{24,28},{28,0},{1,5},{5... | collective-permute-start | bytes 786440 | tf_op jit(solution)/shard_map/ppermute | solution.py:14
  24.0 10.0 %collective-permute-start.3 = (bf16[256,512]{1,0:T(8,128)(2,1)S(1)}, bf16[256,512]{1,0:T(8,128)(2,1)S(1)}, u32[]{:S(2)}, u32[]{:S(2)}) collective-permute-start(bf16[256,512]{1,0:T(8,128)(2,1)S(1)} %subtract_convert_fusion.5), channel_id=1, source_target_pairs={{0,4},{4,8},{8,12},{12,16},{16,20},{20,24},{24,28},{28,0},{1,5},{5... | collective-permute-start | bytes 786440 | tf_op jit(solution)/shard_map/ppermute | solution.py:14
  29.1 11.9 %collective-permute-start.2 = (bf16[256,512]{1,0:T(8,128)(2,1)S(1)}, bf16[256,512]{1,0:T(8,128)(2,1)S(1)}, u32[]{:S(2)}, u32[]{:S(2)}) collective-permute-start(bf16[256,512]{1,0:T(8,128)(2,1)S(1)} %subtract_convert_fusion.6), channel_id=1, source_target_pairs={{0,4},{4,8},{8,12},{12,16},{16,20},{20,24},{24,28},{28,0},{1,5},{5... | collective-permute-start | bytes 786440 | tf_op jit(solution)/shard_map/ppermute | solution.py:14
  34.7 16.8 %collective-permute-start.5 = (bf16[256,512]{1,0:T(8,128)(2,1)S(1)}, bf16[256,512]{1,0:T(8,128)(2,1)S(1)}, u32[]{:S(2)}, u32[]{:S(2)}) collective-permute-start(bf16[256,512]{1,0:T(8,128)(2,1)S(1)} %subtract_convert_fusion.3), channel_id=1, source_target_pairs={{0,4},{4,8},{8,12},{12,16},{16,20},{20,24},{24,28},{28,0},{1,5},{5... | collective-permute-start | bytes 786440 | tf_op jit(solution)/shard_map/ppermute | solution.py:14
  41.7 9.1 %collective-permute-start.4 = (bf16[256,512]{1,0:T(8,128)(2,1)S(1)}, bf16[256,512]{1,0:T(8,128)(2,1)S(1)}, u32[]{:S(2)}, u32[]{:S(2)}) collective-permute-start(bf16[256,512]{1,0:T(8,128)(2,1)S(1)} %subtract_convert_fusion.4), channel_id=1, source_target_pairs={{0,4},{4,8},{8,12},{12,16},{16,20},{20,24},{24,28},{28,0},{1,5},{5... | collective-permute-start | bytes 786440 | tf_op jit(solution)/shard_map/ppermute | solution.py:14
Sparse Core Ops, SparseCore 0:
  54.6 20.7 all-gather.2
